TPU v7x, 32 devices: a whole 2x2x4 slice. The times are simulated.
32 devices in a mesh: kpt: 2 (over y), ga: 16 (over z, x, core).
Axes of the slice: x: 2, y: 2, z: 4, core: 2. Of those that a mesh axis runs over, the one named last changes fastest.
Arguments:
- miller_index: int32 [3, 12288], P(None, 'ga'), may hold values from -12 to 12
- kpoint: float32 [6], P('kpt'), parts along dimension 0, may hold values from -0.5 to 0.5
- waves: bfloat16 [2, 256, 12288], P(None, 'kpt', 'ga'), parts along dimension 1, may hold values from -6 to 6
- species: int32 [16], replicated, may hold values from 0 to 3
- counts: int32 [16], replicated, may hold values from 1 to 8
- positions: int32 [3, 16], replicated, may hold values from 0 to 63
- radial_coef: float32 [4, 8, 16], replicated, may hold values from -4 to 4
- coupling: float32 [16, 8, 8], replicated, as said below
Outputs:
- applied: bfloat16 [2, 256, 12288], P(None, 'kpt', 'ga'), parts along dimension 1
- energy: float32 [256], P('kpt'), parts along dimension 0
There are 2 independent parts, one for each index of `kpt`. A program takes and returns all parts, laid end to end along the dimension named above; an argument that names none is the same for every part. Nothing has to cross between parts.
Inputs may be any that keep to these rules, and one draw needn't show every extreme that they name: `coupling`: symmetric in its last two dimensions.
All inputs are finite; a program needn't handle non-finite values.
Results may differ from a plain program's by a relative error of at most 0.0062.
Values may be sent and summed in bfloat16 or wider, within the bound.
A program may use at most 64 MiB of HBM per device.

v0:
```python
import math

import jax
import jax.numpy as jnp
from jax import lax
from jax.sharding import PartitionSpec as P

PROJ = 8
MGRID = 64
ATOM_BLOCK = 16


def prepare(miller_index, kpoint, terms):
    shifted = miller_index.astype(jnp.float32) + kpoint[:, None]
    squared = jnp.sum(shifted * shifted, axis=0)
    widths = 0.001 * 1.5 ** jnp.arange(terms).astype(jnp.float32)
    basis = jnp.exp(-widths[:, None] * squared[None, :])
    angular = jnp.concatenate(
        [jnp.ones_like(squared)[None], shifted / jnp.sqrt(squared + 1.0)[None]], 0
    )
    angular = jnp.concatenate([angular, angular], 0)
    return (basis, angular)


def projectors(
    first, miller_index, kpoint, basis, angular, species, counts, positions, radial_coef, scaling
):
    kinds = lax.dynamic_slice_in_dim(species, first, ATOM_BLOCK)
    numbers = lax.dynamic_slice_in_dim(counts, first, ATOM_BLOCK)
    places = lax.dynamic_slice_in_dim(positions, first, ATOM_BLOCK, 1)
    selector = (kinds[:, None] == jnp.arange(radial_coef.shape[0])[None, :]).astype(jnp.float32)
    chosen = jnp.einsum("as,sjr->ajr", selector, radial_coef, precision=lax.Precision.HIGHEST)
    radial = jnp.einsum("ajr,rg->ajg", chosen, basis, precision=lax.Precision.HIGHEST)
    active = (jnp.arange(PROJ)[None, :] < numbers[:, None]).astype(jnp.float32)
    amplitude = radial * angular[None] * active[:, :, None] * scaling
    winding = jnp.mod(jnp.sum(miller_index[:, None, :] * places[:, :, None], axis=0), MGRID)
    offset = jnp.sum(kpoint[:, None] * places.astype(jnp.float32), axis=0)
    phase = 2.0 * math.pi / MGRID * (winding.astype(jnp.float32) + offset[:, None])
    planes = miller_index.shape[1]
    real_part = (
        (amplitude * jnp.cos(phase)[:, None, :])
        .astype(jnp.bfloat16)
        .reshape(ATOM_BLOCK * PROJ, planes)
    )
    imag_part = (
        (-amplitude * jnp.sin(phase)[:, None, :])
        .astype(jnp.bfloat16)
        .reshape(ATOM_BLOCK * PROJ, planes)
    )
    return (real_part, imag_part)


def measure(real_part, imag_part, coeffs):
    over_re = jnp.einsum(
        "sg,bg->sb", real_part, coeffs[0], preferred_element_type=jnp.float32
    ) + jnp.einsum("sg,bg->sb", imag_part, coeffs[1], preferred_element_type=jnp.float32)
    over_im = jnp.einsum(
        "sg,bg->sb", real_part, coeffs[1], preferred_element_type=jnp.float32
    ) - jnp.einsum("sg,bg->sb", imag_part, coeffs[0], preferred_element_type=jnp.float32)
    return jnp.stack([over_re, over_im])


def spread(rows, real_part, imag_part):
    out_re = jnp.einsum(
        "sb,sg->bg", rows[0], real_part, preferred_element_type=jnp.float32
    ) - jnp.einsum("sb,sg->bg", rows[1], imag_part, preferred_element_type=jnp.float32)
    out_im = jnp.einsum(
        "sb,sg->bg", rows[1], real_part, preferred_element_type=jnp.float32
    ) + jnp.einsum("sb,sg->bg", rows[0], imag_part, preferred_element_type=jnp.float32)
    return jnp.stack([out_re, out_im])


def on_device(miller_index, kpoint, waves, species, counts, positions, radial_coef, coupling):
    planes = waves.shape[2]
    bands = waves.shape[1]
    scaling = 1.0 / math.sqrt(planes * lax.axis_size("ga"))
    atoms = coupling.shape[0]
    slots_all = atoms * PROJ
    blocks = atoms // ATOM_BLOCK
    width = ATOM_BLOCK * PROJ
    basis, angular = prepare(miller_index, kpoint, radial_coef.shape[2])

    def build(index):
        return projectors(
            index * ATOM_BLOCK,
            miller_index,
            kpoint,
            basis,
            angular,
            species,
            counts,
            positions,
            radial_coef,
            scaling,
        )

    empty = jnp.zeros((2, bands, planes), jnp.float32)

    def first_pass(index, table):
        real_part, imag_part = build(index)
        return lax.dynamic_update_slice_in_dim(
            table, measure(real_part, imag_part, waves), index * width, 1
        )

    local = lax.fori_loop(0, blocks, first_pass, jnp.zeros((2, slots_all, bands), jnp.float32))
    summed = lax.psum(local, "ga")
    shaped = summed.reshape(2, atoms, PROJ, summed.shape[2])
    weighted = jnp.einsum("aij,cajb->caib", coupling, shaped, precision=lax.Precision.HIGHEST)
    weighted = weighted.reshape(2, atoms * PROJ, summed.shape[2])
    energy = jnp.sum(summed * weighted, axis=(0, 1))
    table = weighted.astype(jnp.bfloat16)

    def second_pass(index, output):
        real_part, imag_part = build(index)
        rows = lax.dynamic_slice_in_dim(table, index * width, width, 1)
        return output + spread(rows, real_part, imag_part)

    output = lax.fori_loop(0, blocks, second_pass, empty)
    return (output.astype(jnp.bfloat16), energy / slots_all)


def solution(mesh):
    in_specs = (P(None, "ga"), P("kpt"), P(None, "kpt", "ga"), P(), P(), P(), P(), P())
    out_specs = (P(None, "kpt", "ga"), P("kpt"))
    return jax.shard_map(
        on_device, mesh=mesh, in_specs=in_specs, out_specs=out_specs, check_vma=False
    )
```

profile of v0, /device:TPU:0, one launch (start us, length us, event | category | flops | bytes accessed | tf_op | source)
XLA Modules:
  0.0 116.0 jit_solution(3049479459820801523)
XLA Ops:
  7.3 0.6 copy-done.6
  7.8 0.8 multiply_reduce_fusion.2
  8.6 0.8 multiply_reduce_fusion.1
  9.6 0.6 copy-done.8
  10.3 0.3 fusion.40
  10.6 0.4 copy-done.7
  10.9 0.2 fusion.33
  11.2 0.6 fusion.8
  11.8 0.4 copy-done.1
  12.2 0.2 fusion.9
  12.4 0.2 fusion.13
  12.6 0.2 fusion.5
  12.8 0.2 fusion.6
  13.1 0.7 pad_maximum_fusion.1
  13.8 0.7 copy-done.4
  14.6 90.4 %all-reduce.2.cloned.1.call-done = f32[2,128,128]{2,1,0:T(8,128)} async-done(((f32[2,128,128]{2,1,0:T(8,128)}), f32[2,128,128]{2,1,0:T(8,128)}) %all-reduce.2.cloned.1.call-update) | async-done | bytes 131088 | tf_op jit(solution)/shard_map/psum | solution.py:106
  105.0 1.1 convolution_bitcast_fusion
  106.2 0.2 fusion.30
  106.4 0.2 fusion.29
  106.6 0.7 copy-done.2
  107.4 0.5 broadcast_multiply_fusion
  107.9 0.2 fusion.3
  108.1 0.2 fusion.4
  108.4 0.8 pad_maximum_fusion
  (24 shorter events, 0.5 us)
Async XLA Ops:
  7.2 3.4 %copy-start = (f32[4,8,16]{2,1,0:T(8,128)S(1)}, f32[4,8,16]{2,1,0:T(8,128)}, u32[]{:S(2)}) copy-start(f32[4,8,16]{2,1,0:T(8,128)} %param.14) | copy-start | bytes 6148
  7.2 0.7 copy-start.6
  7.2 2.2 %copy-start.3 = (s32[3,768]{1,0:T(4,128)S(1)}, s32[3,768]{1,0:T(4,128)}, u32[]{:S(2)}) copy-start(s32[3,768]{1,0:T(4,128)} %param.8) | copy-start | bytes 27652
  7.2 97.8 %all-reduce.2.cloned.1.call-start = ((), (), s32[]{:S(2)}) async-start(), calls=%async_computation | async-start | bytes 262144 | tf_op jit(solution)/shard_map/psum | solution.py:106
  8.6 0.8 copy-start.5
  9.5 0.7 copy-start.8
  10.3 0.7 copy-start.7
  11.2 1.0 copy-start.1
  13.7 0.8 copy-start.4
  106.4 0.9 copy-start.2
Sparse Core Ops, SparseCore 0:
  13.9 91.0 all-reduce.1
where the time goes:
time: 117 us; the launch traced here: 116 us
  waiting for transfers between devices  90.4 us (77%)
  between operations  14.2 us (12%)
  other arithmetic  4.1 us (4%)
  matrix products  3.75 us (3%)
  local copies, waits for them, and re-layouts  3.44 us (3%)
    psum x1, waiting for transfers between devices, on_device(): summed = lax.psum(local, 'ga')  90.4 us
    unnamed x19, local copies, waits for them, and re-layouts  3.42 us
  transfers between devices with their start and end apart: 1, of which 1 were waited for; matrix products, arithmetic and copies ran while one was open for 0% of the time, Pallas kernels for 0%

commit v1 on v0

v1 whole, which is shorter than its diff:
```python
import functools
import math

import jax
import jax.numpy as jnp
import numpy as np
from jax import lax
from jax.experimental import pallas as pl
from jax.experimental.pallas import tpu as pltpu
from jax.sharding import PartitionSpec as P

PROJ = 8
MGRID = 64
ATOM_BLOCK = 16


def turn_polynomials(degree=8):
    nodes = 0.125 * (1.0 + np.cos(np.pi * (np.arange(200) + 0.5) / 200))
    root = np.sqrt(nodes)
    sine = np.polynomial.Chebyshev.fit(nodes, np.sin(2 * np.pi * root) / root, degree, domain=[0, 0.25])
    cosine = np.polynomial.Chebyshev.fit(nodes, np.cos(2 * np.pi * root), degree, domain=[0, 0.25])
    kind = np.polynomial.Polynomial
    return [[float(c) for c in p.convert(kind=kind).coef] for p in (sine, cosine)]


SINE, COSINE = turn_polynomials()


def horner(coefs, x):
    total = coefs[-1]
    for c in coefs[-2::-1]:
        total = total * x + c
    return total


def peers_of(me, n, body):
    if n <= 32:
        order = sorted(range(1, n), key=lambda k: -min(k, n - k))
        for k in order:
            body(lax.rem(me + k, n))
    else:
        lax.fori_loop(1, n, lambda k, c: (body(lax.rem(me + k, n)), c)[1], 0)


def loop(count, body):
    if count == 1:
        body(0)
    else:
        lax.fori_loop(0, count, lambda i, c: (body(i), c)[1], 0)


def kernel(
    n,
    scaling,
    miller_ref,
    kpoint_ref,
    waves_ref,
    species_ref,
    counts_ref,
    positions_ref,
    radial_ref,
    coupling_ref,
    out_ref,
    energy_ref,
    vbuf,
    bbuf,
    trig,
    table,
    part,
    send,
    recv,
    wbuf,
    ebuf,
    obuf,
    wave_sem,
    out_sem,
    send_sems,
    recv_sems,
):
    me = lax.axis_index("ga")
    atoms = coupling_ref.shape[2]
    own = atoms // n
    bands = waves_ref.shape[1]
    planes = waves_ref.shape[2]
    species_n, _, terms = radial_ref.shape
    f32 = jnp.float32

    wave_copy = pltpu.make_async_copy(waves_ref, vbuf, wave_sem)
    wave_copy.start()
    barrier = pltpu.get_barrier_semaphore()

    def greet(peer):
        pl.semaphore_signal(
            barrier, inc=1, device_id={"ga": peer}, device_id_type=pl.DeviceIdType.MESH
        )

    peers_of(me, n, greet)

    millers = [miller_ref[c : c + 1, :].astype(f32) for c in range(3)]
    shifted = [millers[c] + kpoint_ref[c] for c in range(3)]
    squared = shifted[0] * shifted[0] + shifted[1] * shifted[1] + shifted[2] * shifted[2]
    row = lax.broadcasted_iota(jnp.int32, (PROJ, planes), 0)
    inverse = 1.0 / jnp.sqrt(squared + 1.0)
    kind = lax.rem(row, 4)
    angular = jnp.full((PROJ, planes), scaling, f32)
    for c in range(3):
        angular = jnp.where(kind == c + 1, shifted[c] * inverse * scaling, angular)
    sums = [jnp.zeros((PROJ, planes), f32) for _ in range(species_n)]
    coefs = [radial_ref[s] for s in range(species_n)]
    for r in range(terms):
        width = float(np.float32(0.001) * np.float32(1.5) ** np.float32(r))
        basis = jnp.exp(-width * squared)
        for s in range(species_n):
            sums[s] = sums[s] + coefs[s][:, r : r + 1] * basis
    for s in range(species_n):
        table[s] = sums[s] * angular

    recv[pl.ds(me * own, own)] = jnp.zeros((own, 2 * PROJ, bands), recv.dtype)

    def build(block):
        first = block * ATOM_BLOCK
        diagonal = lax.broadcasted_iota(jnp.int32, (ATOM_BLOCK, atoms), 0) + first
        diagonal = diagonal == lax.broadcasted_iota(jnp.int32, (ATOM_BLOCK, atoms), 1)
        winding = jnp.zeros((ATOM_BLOCK, planes), f32)
        offset = jnp.zeros((ATOM_BLOCK, 1), f32)
        for c in range(3):
            places = positions_ref[c : c + 1, :].astype(f32)
            column = jnp.sum(jnp.where(diagonal, places, 0.0), axis=1, keepdims=True)
            winding = winding + column * millers[c]
            offset = offset + column * kpoint_ref[c]
        winding = winding - MGRID * jnp.floor(winding * (1.0 / MGRID))
        turns = (winding + offset) * (1.0 / MGRID)
        turns = turns - jnp.floor(turns + 0.5)
        square = turns * turns
        trig[0] = horner(COSINE, square)
        trig[1] = -(turns * horner(SINE, square))
        for a in range(ATOM_BLOCK):
            live = row < counts_ref[first + a]
            amplitude = jnp.where(live, table[species_ref[first + a]], 0.0)
            both = jnp.concatenate(
                [amplitude * trig[0, a : a + 1, :], amplitude * trig[1, a : a + 1, :]], axis=0
            )
            at = (first + a) * (2 * PROJ)
            if not isinstance(at, int):
                at = pl.multiple_of(at, 2 * PROJ)
            bbuf[pl.ds(at, 2 * PROJ), :] = both.astype(bbuf.dtype)

    loop(atoms // ATOM_BLOCK, build)
    wave_copy.wait()
    height = ATOM_BLOCK * 2 * PROJ

    def intersect(block):
        at = block * height
        if not isinstance(at, int):
            at = pl.multiple_of(at, height)
        product = lax.dot_general(
            bbuf[pl.ds(at, height), :],
            vbuf[...].reshape(2 * bands, planes),
            (((1,), (1,)), ((), ())),
            preferred_element_type=f32,
        )
        product = product.reshape(ATOM_BLOCK, 2, PROJ, 2 * bands)
        over_re = product[:, 0, :, :bands] + product[:, 1, :, bands:]
        over_im = product[:, 0, :, bands:] - product[:, 1, :, :bands]
        over = jnp.concatenate([over_re, over_im], axis=1)
        part[pl.ds(block * ATOM_BLOCK, ATOM_BLOCK)] = over
        send[pl.ds(block * ATOM_BLOCK, ATOM_BLOCK)] = over.astype(send.dtype)

    loop(atoms // ATOM_BLOCK, intersect)
    pl.semaphore_wait(barrier, n - 1)

    def scatter(peer):
        pltpu.make_async_remote_copy(
            src_ref=send.at[pl.ds(peer * own, own)],
            dst_ref=recv.at[pl.ds(me * own, own)],
            send_sem=send_sems.at[0],
            recv_sem=recv_sems.at[0],
            device_id={"ga": peer},
            device_id_type=pl.DeviceIdType.MESH,
        ).start()

    peers_of(me, n, scatter)

    columns = []
    for k in range(own):
        mine = lax.broadcasted_iota(jnp.int32, (PROJ, atoms), 1) == me * own + k
        columns.append(
            [
                jnp.broadcast_to(
                    jnp.sum(jnp.where(mine, coupling_ref[j], 0.0), axis=1, keepdims=True),
                    (PROJ, bands),
                )
                for j in range(PROJ)
            ]
        )

    def all_of(ref, sem):
        view = ref.at[pl.ds(0, ref.shape[0] // n * (n - 1))]
        return pltpu.make_async_copy(view, view, sem)

    all_of(recv, recv_sems.at[0]).wait()
    energy = jnp.zeros((1, bands), f32)
    for k in range(own):
        over = part[me * own + k]
        for p in range(n):
            over = over + recv[p * own + k].astype(f32)
        weighted = []
        for half in range(2):
            piece = over[half * PROJ : (half + 1) * PROJ]
            total = columns[k][0] * piece[0:1]
            for j in range(1, PROJ):
                total = total + columns[k][j] * piece[j : j + 1]
            energy = energy + jnp.sum(total * piece, axis=0, keepdims=True)
            weighted.append(total)
        wbuf[me * own + k] = jnp.concatenate(weighted, axis=0).astype(wbuf.dtype)
    ebuf[me] = energy

    def gather(peer):
        pltpu.make_async_remote_copy(
            src_ref=wbuf.at[pl.ds(me * own, own)],
            dst_ref=wbuf.at[pl.ds(me * own, own)],
            send_sem=send_sems.at[1],
            recv_sem=recv_sems.at[1],
            device_id={"ga": peer},
            device_id_type=pl.DeviceIdType.MESH,
        ).start()

    def gather_energy(peer):
        pltpu.make_async_remote_copy(
            src_ref=ebuf.at[me],
            dst_ref=ebuf.at[me],
            send_sem=send_sems.at[2],
            recv_sem=recv_sems.at[2],
            device_id={"ga": peer},
            device_id_type=pl.DeviceIdType.MESH,
        ).start()

    peers_of(me, n, gather)
    peers_of(me, n, gather_energy)
    all_of(send, send_sems.at[0]).wait()
    all_of(wbuf, recv_sems.at[1]).wait()

    weights = wbuf[...].astype(f32)
    upper, lower = weights[:, :PROJ], weights[:, PROJ:]
    halves = (
        jnp.concatenate([upper, -lower], axis=1),
        jnp.concatenate([lower, upper], axis=1),
    )
    copies = []
    for half in range(2):
        matrix = halves[half].astype(bbuf.dtype).reshape(atoms * 2 * PROJ, bands)
        obuf[half] = lax.dot_general(
            matrix, bbuf[...], (((0,), (0,)), ((), ())), preferred_element_type=f32
        ).astype(obuf.dtype)
        copies.append(pltpu.make_async_copy(obuf.at[half], out_ref.at[half], out_sem.at[half]))
        copies[-1].start()
    all_of(ebuf, recv_sems.at[2]).wait()
    energy_ref[...] = jnp.sum(ebuf[...], axis=(0, 1)) / (atoms * PROJ)
    all_of(wbuf, send_sems.at[1]).wait()
    all_of(ebuf, send_sems.at[2]).wait()
    for copy in copies:
        copy.wait()


def on_device(miller_index, kpoint, waves, species, counts, positions, radial_coef, coupling):
    n = lax.axis_size("ga")
    _, bands, planes = waves.shape
    atoms = coupling.shape[0]
    scaling = 1.0 / math.sqrt(planes * n)
    vmem = pl.BlockSpec(memory_space=pltpu.VMEM)
    smem = pl.BlockSpec(memory_space=pltpu.SMEM)
    anywhere = pl.BlockSpec(memory_space=pl.ANY)
    bf16, f32 = jnp.bfloat16, jnp.float32
    applied, energy = pl.pallas_call(
        functools.partial(kernel, n, scaling),
        out_shape=(
            jax.ShapeDtypeStruct((2, bands, planes), bf16),
            jax.ShapeDtypeStruct((bands,), f32),
        ),
        in_specs=[vmem, smem, anywhere, smem, smem, vmem, vmem, vmem],
        out_specs=(anywhere, vmem),
        scratch_shapes=[
            pltpu.VMEM((2, bands, planes), bf16),
            pltpu.VMEM((atoms * 2 * PROJ, planes), bf16),
            pltpu.VMEM((2, ATOM_BLOCK, planes), f32),
            pltpu.VMEM((radial_coef.shape[0], PROJ, planes), f32),
            pltpu.VMEM((atoms, 2 * PROJ, bands), f32),
            pltpu.VMEM((atoms, 2 * PROJ, bands), bf16),
            pltpu.VMEM((atoms, 2 * PROJ, bands), bf16),
            pltpu.VMEM((atoms, 2 * PROJ, bands), bf16),
            pltpu.VMEM((n, 1, bands), f32),
            pltpu.VMEM((2, bands, planes), bf16),
            pltpu.SemaphoreType.DMA,
            pltpu.SemaphoreType.DMA((2,)),
            pltpu.SemaphoreType.DMA((3,)),
            pltpu.SemaphoreType.DMA((3,)),
        ],
        compiler_params=pltpu.CompilerParams(collective_id=0, has_side_effects=True),
    )(
        miller_index,
        kpoint,
        waves,
        species,
        counts,
        positions,
        radial_coef,
        jnp.transpose(coupling, (2, 1, 0)),
    )
    return applied, energy


def solution(mesh):
    in_specs = (P(None, "ga"), P("kpt"), P(None, "kpt", "ga"), P(), P(), P(), P(), P())
    out_specs = (P(None, "kpt", "ga"), P("kpt"))
    return jax.shard_map(
        on_device, mesh=mesh, in_specs=in_specs, out_specs=out_specs, check_vma=False
    )
```

time: 117 us -> 22.2 us (0.19)
  waiting for transfers between devices: 90.4 us -> 0 us
  Pallas kernels: 0 us -> 17.5 us
  between operations: 14.2 us -> 0.65 us
  other arithmetic: 4.1 us -> 0 us
  matrix products: 3.75 us -> 0 us
    psum x1 -> x0, waiting for transfers between devices: 90.4 us -> none  [on_device(): summed = lax.psum(local, 'ga')]
    pallas_call x0 -> x1, Pallas kernels: none -> 17.5 us  [on_device(): pl.pallas_call(functools.partial(kernel, n, scaling), out_shape=(jax.Shap...]
    dot_general x11 -> x0, matrix products: 3.75 us -> none  [the longest x1 1.14 us: on_device(): jnp.einsum('aij,cajb->caib', coupling, shaped, precision=lax.Precision.HI...]
    reduce_sum x4 -> x0, other arithmetic: 1.7 us -> none  [the longest x1 0.8 us: prepare(): squared = jnp.sum(shifted * shifted, axis=0)]
    another operation x2 -> x0, other arithmetic: 1.45 us -> none  [the longest x1 0.78 us: spread(): return jnp.stack([out_re, out_im])]
    unnamed x19 -> x5, local copies, waits for them, and re-layouts: 3.42 us -> 3.66 us
  transfers between devices with their start and end apart: 1 -> 0, of which waited for: 1 -> 0; matrix products, arithmetic and copies ran while one was open for 0% -> 0% of each run, Pallas kernels for 0% -> 0%
where the time goes in v1:
time: 22.2 us; the launch traced here: 21.9 us
  Pallas kernels  17.5 us (79%)
  local copies, waits for them, and re-layouts  3.66 us (16%)
  between operations  0.65 us (3%)
    pallas_call x1, Pallas kernels, on_device(): pl.pallas_call(functools.partial(kernel, n, scaling), out_shape=(jax.Shap...  17.5 us
    unnamed x5, local copies, waits for them, and re-layouts  3.66 us

profile of v1, /device:TPU:0, one launch (start us, length us, event | category | flops | bytes accessed | tf_op | source)
XLA Modules:
  0.0 21.9 jit_solution(5372144709220262669)
XLA Ops:
  0.6 1.4 %copy.12 = f32[16,8,8]{0,1,2:T(8,128)} copy(f32[16,8,8]{0,2,1:T(8,128)} %param.15) | data formatting | bytes 8192 | tf_op args[7]
  2.0 17.5 %shard_map.95 = (bf16[2,128,768]{2,1,0:T(8,128)(2,1)}, f32[128]{0:T(128)}) custom-call(s32[3,768]{1,0:T(4,128)} %miller_ref.1, f32[3]{0:T(128)} %kpoint_ref.1, bf16[2,128,768]{2,1,0:T(8,128)(2,1)} %waves_ref.1, s32[16]{0:T(128)} %species_ref.1, s32[16]{0:T(128)} %counts_ref.1, s32[3,16]{1,0:T(4,128)} %positions_ref.1, f32[4,8,16]{2,1,0:T(8,128)} %radial_ref.1, ...), custom_call_target="tpu_custom_call" | custom-call | tf_op jit(solution)/shard_map/pallas_call | solution.py:274
  19.6 0.0 copy-start
  19.6 1.8 %copy.15 = bf16[2,128,768]{2,1,0:T(8,128)(2,1)} copy(bf16[2,128,768]{2,1,0:T(8,128)(2,1)} %get-tuple-element.4) | data formatting | bytes 786432
  21.3 0.0 copy-done
  21.3 0.5 %copy.16 = f32[128]{0:T(128)} copy(f32[128]{0:T(128)S(1)} %copy-done) | data formatting | bytes 1024
Async XLA Ops:
  19.6 1.8 %copy-start = (f32[128]{0:T(128)S(1)}, f32[128]{0:T(128)}, u32[]{:S(2)}) copy-start(f32[128]{0:T(128)} %get-tuple-element.5) | copy-start | bytes 1540

commit v2 on v1

--- a/solution.py
+++ b/solution.py
@@ -33,6 +33,12 @@
     return total
 
 
+def owners_of(n, atoms):
+    if n % 4 == 0 and atoms % (n // 4) == 0:
+        return n // 4, 1, 2
+    return n, 0, 1
+
+
 def peers_of(me, n, body):
     if n <= 32:
         order = sorted(range(1, n), key=lambda k: -min(k, n - k))
@@ -42,6 +48,14 @@
         lax.fori_loop(1, n, lambda k, c: (body(lax.rem(me + k, n)), c)[1], 0)
 
 
+def repeat(count, body):
+    if count <= 32:
+        for k in range(count):
+            body(k)
+    else:
+        lax.fori_loop(0, count, lambda k, c: (body(k), c)[1], 0)
+
+
 def loop(count, body):
     if count == 1:
         body(0)
@@ -52,14 +66,14 @@
 def kernel(
     n,
     scaling,
-    miller_ref,
-    kpoint_ref,
+    miller_hbm,
+    kpoint_hbm,
     waves_ref,
-    species_ref,
-    counts_ref,
-    positions_ref,
-    radial_ref,
-    coupling_ref,
+    species_hbm,
+    counts_hbm,
+    positions_hbm,
+    radial_hbm,
+    coupling_hbm,
     out_ref,
     energy_ref,
     vbuf,
@@ -71,20 +85,43 @@
     recv,
     wbuf,
     ebuf,
-    obuf,
+    tally,
     wave_sem,
-    out_sem,
     send_sems,
     recv_sems,
+    miller_ref,
+    kpoint_ref,
+    species_ref,
+    counts_ref,
+    positions_ref,
+    radial_ref,
+    coupling_ref,
+    load_sems,
 ):
     me = lax.axis_index("ga")
-    atoms = coupling_ref.shape[2]
-    own = atoms // n
+    atoms = coupling_hbm.shape[2]
+    q, base, stride = owners_of(n, atoms)
+    own = atoms // q
+    rank = (me - base) // stride
+    is_owner = (me >= base) & (rank < q) & (lax.rem(me - base + n * stride, stride) == 0)
+    mine_rank = jnp.clip(rank, 0, q - 1)
     bands = waves_ref.shape[1]
     planes = waves_ref.shape[2]
-    species_n, _, terms = radial_ref.shape
+    species_n, _, terms = radial_hbm.shape
     f32 = jnp.float32
 
+    pairs = (
+        (miller_hbm, miller_ref),
+        (kpoint_hbm, kpoint_ref),
+        (species_hbm, species_ref),
+        (counts_hbm, counts_ref),
+        (positions_hbm, positions_ref),
+        (radial_hbm, radial_ref),
+        (coupling_hbm, coupling_ref),
+    )
+    loads = [pltpu.make_async_copy(a, b, load_sems.at[i]) for i, (a, b) in enumerate(pairs)]
+    for load in loads:
+        load.start()
     wave_copy = pltpu.make_async_copy(waves_ref, vbuf, wave_sem)
     wave_copy.start()
     barrier = pltpu.get_barrier_semaphore()
@@ -96,6 +133,8 @@
 
     peers_of(me, n, greet)
 
+    for load in loads:
+        load.wait()
     millers = [miller_ref[c : c + 1, :].astype(f32) for c in range(3)]
     shifted = [millers[c] + kpoint_ref[c] for c in range(3)]
     squared = shifted[0] * shifted[0] + shifted[1] * shifted[1] + shifted[2] * shifted[2]
@@ -114,8 +153,6 @@
             sums[s] = sums[s] + coefs[s][:, r : r + 1] * basis
     for s in range(species_n):
         table[s] = sums[s] * angular
-
-    recv[pl.ds(me * own, own)] = jnp.zeros((own, 2 * PROJ, bands), recv.dtype)
 
     def build(block):
         first = block * ATOM_BLOCK
@@ -169,97 +206,109 @@
     loop(atoms // ATOM_BLOCK, intersect)
     pl.semaphore_wait(barrier, n - 1)
 
-    def scatter(peer):
-        pltpu.make_async_remote_copy(
-            src_ref=send.at[pl.ds(peer * own, own)],
-            dst_ref=recv.at[pl.ds(me * own, own)],
-            send_sem=send_sems.at[0],
-            recv_sem=recv_sems.at[0],
-            device_id={"ga": peer},
-            device_id_type=pl.DeviceIdType.MESH,
-        ).start()
-
-    peers_of(me, n, scatter)
-
-    columns = []
-    for k in range(own):
-        mine = lax.broadcasted_iota(jnp.int32, (PROJ, atoms), 1) == me * own + k
-        columns.append(
-            [
-                jnp.broadcast_to(
-                    jnp.sum(jnp.where(mine, coupling_ref[j], 0.0), axis=1, keepdims=True),
-                    (PROJ, bands),
-                )
-                for j in range(PROJ)
-            ]
-        )
-
-    def all_of(ref, sem):
-        view = ref.at[pl.ds(0, ref.shape[0] // n * (n - 1))]
+    def many_of(ref, count, sem):
+        view = ref.at[pl.ds(0, count)]
         return pltpu.make_async_copy(view, view, sem)
 
-    all_of(recv, recv_sems.at[0]).wait()
-    energy = jnp.zeros((1, bands), f32)
-    for k in range(own):
-        over = part[me * own + k]
-        for p in range(n):
-            over = over + recv[p * own + k].astype(f32)
-        weighted = []
-        for half in range(2):
-            piece = over[half * PROJ : (half + 1) * PROJ]
-            total = columns[k][0] * piece[0:1]
-            for j in range(1, PROJ):
-                total = total + columns[k][j] * piece[j : j + 1]
-            energy = energy + jnp.sum(total * piece, axis=0, keepdims=True)
-            weighted.append(total)
-        wbuf[me * own + k] = jnp.concatenate(weighted, axis=0).astype(wbuf.dtype)
-    ebuf[me] = energy
-
-    def gather(peer):
-        pltpu.make_async_remote_copy(
-            src_ref=wbuf.at[pl.ds(me * own, own)],
-            dst_ref=wbuf.at[pl.ds(me * own, own)],
-            send_sem=send_sems.at[1],
-            recv_sem=recv_sems.at[1],
-            device_id={"ga": peer},
-            device_id_type=pl.DeviceIdType.MESH,
-        ).start()
-
-    def gather_energy(peer):
-        pltpu.make_async_remote_copy(
-            src_ref=ebuf.at[me],
-            dst_ref=ebuf.at[me],
-            send_sem=send_sems.at[2],
-            recv_sem=recv_sems.at[2],
-            device_id={"ga": peer},
-            device_id_type=pl.DeviceIdType.MESH,
-        ).start()
-
-    peers_of(me, n, gather)
-    peers_of(me, n, gather_energy)
-    all_of(send, send_sems.at[0]).wait()
-    all_of(wbuf, recv_sems.at[1]).wait()
-
-    weights = wbuf[...].astype(f32)
+    def scatter(o):
+        peer = base + o * stride
+
+        @pl.when(peer != me)
+        def _():
+            pltpu.make_async_remote_copy(
+                src_ref=send.at[pl.ds(o * own, own)],
+                dst_ref=recv.at[me],
+                send_sem=send_sems.at[0],
+                recv_sem=recv_sems.at[0],
+                device_id={"ga": peer},
+                device_id_type=pl.DeviceIdType.MESH,
+            ).start()
+
+    repeat(q, scatter)
+
+    @pl.when(is_owner)
+    def _():
+        recv[me] = jnp.zeros((own, 2 * PROJ, bands), recv.dtype)
+        columns = []
+        for k in range(own):
+            mine = lax.broadcasted_iota(jnp.int32, (PROJ, atoms), 1) == mine_rank * own + k
+            columns.append(
+                [
+                    jnp.broadcast_to(
+                        jnp.sum(jnp.where(mine, coupling_ref[j], 0.0), axis=1, keepdims=True),
+                        (PROJ, bands),
+                    )
+                    for j in range(PROJ)
+                ]
+            )
+        many_of(recv, n - 1, recv_sems.at[0]).wait()
+        energy = jnp.zeros((1, bands), f32)
+        for k in range(own):
+            over = part[mine_rank * own + k]
+            for p in range(n):
+                over = over + recv[p, k].astype(f32)
+            weighted = []
+            for half in range(2):
+                piece = over[half * PROJ : (half + 1) * PROJ]
+                total = columns[k][0] * piece[0:1]
+                for j in range(1, PROJ):
+                    total = total + columns[k][j] * piece[j : j + 1]
+                energy = energy + jnp.sum(total * piece, axis=0, keepdims=True)
+                weighted.append(total)
+            wbuf[mine_rank, k] = jnp.concatenate(weighted, axis=0).astype(wbuf.dtype)
+        ebuf[mine_rank] = energy
+
+        def spread(buffer, index):
+            def copy(peer):
+                pltpu.make_async_remote_copy(
+                    src_ref=buffer.at[mine_rank],
+                    dst_ref=buffer.at[mine_rank],
+                    send_sem=send_sems.at[index],
+                    recv_sem=recv_sems.at[index],
+                    device_id={"ga": peer},
+                    device_id_type=pl.DeviceIdType.MESH,
+                ).start()
+
+            return copy
+
+        peers_of(me, n, spread(wbuf, 1))
+        peers_of(me, n, spread(ebuf, 2))
+        many_of(send, (q - 1) * own, send_sems.at[0]).wait()
+        if q > 1:
+            many_of(wbuf, q - 1, recv_sems.at[1]).wait()
+
+    @pl.when(jnp.logical_not(is_owner))
+    def _():
+        many_of(send, q * own, send_sems.at[0]).wait()
+        many_of(wbuf, q, recv_sems.at[1]).wait()
+
+    weights = wbuf[...].reshape(atoms, 2 * PROJ, bands).astype(f32)
     upper, lower = weights[:, :PROJ], weights[:, PROJ:]
     halves = (
         jnp.concatenate([upper, -lower], axis=1),
         jnp.concatenate([lower, upper], axis=1),
     )
-    copies = []
     for half in range(2):
         matrix = halves[half].astype(bbuf.dtype).reshape(atoms * 2 * PROJ, bands)
-        obuf[half] = lax.dot_general(
+        out_ref[half] = lax.dot_general(
             matrix, bbuf[...], (((0,), (0,)), ((), ())), preferred_element_type=f32
-        ).astype(obuf.dtype)
-        copies.append(pltpu.make_async_copy(obuf.at[half], out_ref.at[half], out_sem.at[half]))
-        copies[-1].start()
-    all_of(ebuf, recv_sems.at[2]).wait()
+        ).astype(out_ref.dtype)
+
+    @pl.when(is_owner)
+    def _():
+        if q > 1:
+            many_of(ebuf, q - 1, recv_sems.at[2]).wait()
+
+    @pl.when(jnp.logical_not(is_owner))
+    def _():
+        many_of(ebuf, q, recv_sems.at[2]).wait()
+
     energy_ref[...] = jnp.sum(ebuf[...], axis=(0, 1)) / (atoms * PROJ)
-    all_of(wbuf, send_sems.at[1]).wait()
-    all_of(ebuf, send_sems.at[2]).wait()
-    for copy in copies:
-        copy.wait()
+
+    @pl.when(is_owner)
+    def _():
+        for index, buffer in ((1, recv), (2, tally)):
+            many_of(buffer, n - 1, send_sems.at[index]).wait()
 
 
 def on_device(miller_index, kpoint, waves, species, counts, positions, radial_coef, coupling):
@@ -267,6 +316,8 @@
     _, bands, planes = waves.shape
     atoms = coupling.shape[0]
     scaling = 1.0 / math.sqrt(planes * n)
+    q = owners_of(n, atoms)[0]
+    own = atoms // q
     vmem = pl.BlockSpec(memory_space=pltpu.VMEM)
     smem = pl.BlockSpec(memory_space=pltpu.SMEM)
     anywhere = pl.BlockSpec(memory_space=pl.ANY)
@@ -274,11 +325,11 @@
     applied, energy = pl.pallas_call(
         functools.partial(kernel, n, scaling),
         out_shape=(
-            jax.ShapeDtypeStruct((2, bands, planes), bf16),
-            jax.ShapeDtypeStruct((bands,), f32),
+            pltpu.VMEM((2, bands, planes), bf16),
+            pltpu.VMEM((bands,), f32),
         ),
-        in_specs=[vmem, smem, anywhere, smem, smem, vmem, vmem, vmem],
-        out_specs=(anywhere, vmem),
+        in_specs=[anywhere] * 8,
+        out_specs=(vmem, vmem),
         scratch_shapes=[
             pltpu.VMEM((2, bands, planes), bf16),
             pltpu.VMEM((atoms * 2 * PROJ, planes), bf16),
@@ -286,14 +337,21 @@
             pltpu.VMEM((radial_coef.shape[0], PROJ, planes), f32),
             pltpu.VMEM((atoms, 2 * PROJ, bands), f32),
             pltpu.VMEM((atoms, 2 * PROJ, bands), bf16),
-            pltpu.VMEM((atoms, 2 * PROJ, bands), bf16),
-            pltpu.VMEM((atoms, 2 * PROJ, bands), bf16),
+            pltpu.VMEM((n, own, 2 * PROJ, bands), bf16),
+            pltpu.VMEM((q, own, 2 * PROJ, bands), bf16),
+            pltpu.VMEM((q, 1, bands), f32),
             pltpu.VMEM((n, 1, bands), f32),
-            pltpu.VMEM((2, bands, planes), bf16),
             pltpu.SemaphoreType.DMA,
-            pltpu.SemaphoreType.DMA((2,)),
             pltpu.SemaphoreType.DMA((3,)),
             pltpu.SemaphoreType.DMA((3,)),
+            pltpu.VMEM(miller_index.shape, jnp.int32),
+            pltpu.SMEM(kpoint.shape, f32),
+            pltpu.SMEM(species.shape, jnp.int32),
+            pltpu.SMEM(counts.shape, jnp.int32),
+            pltpu.VMEM(positions.shape, jnp.int32),
+            pltpu.VMEM(radial_coef.shape, f32),
+            pltpu.VMEM((PROJ, PROJ, atoms), f32),
+            pltpu.SemaphoreType.DMA((7,)),
         ],
         compiler_params=pltpu.CompilerParams(collective_id=0, has_side_effects=True),
     )(
@@ -304,7 +362,7 @@
         counts,
         positions,
         radial_coef,
-        jnp.transpose(coupling, (2, 1, 0)),
+        jnp.transpose(coupling, (1, 2, 0)),
     )
     return applied, energy
 

time: 22.2 us -> 15.6 us (0.70)
  Pallas kernels: 17.5 us -> 13.5 us
  local copies, waits for them, and re-layouts: 3.66 us -> 1.26 us
    pallas_call x1, Pallas kernels: 17.5 us -> 13.5 us  [on_device(): pl.pallas_call(functools.partial(kernel, n, scaling), out_shape=(pltpu.VM...]
    unnamed x5 -> x2, local copies, waits for them, and re-layouts: 3.66 us -> 1.26 us
where the time goes in v2:
time: 15.6 us; the launch traced here: 15.4 us
  Pallas kernels  13.5 us (87%)
  local copies, waits for them, and re-layouts  1.26 us (8%)
  between operations  0.64 us (4%)
    pallas_call x1, Pallas kernels, on_device(): pl.pallas_call(functools.partial(kernel, n, scaling), out_shape=(pltpu.VM...  13.5 us
    unnamed x2, local copies, waits for them, and re-layouts  1.26 us

profile of v2, /device:TPU:0, one launch (start us, length us, event | category | flops | bytes accessed | tf_op | source)
XLA Modules:
  0.0 15.4 jit_solution(6394076573419201056)
XLA Ops:
  0.6 13.5 %shard_map.95 = (bf16[2,128,768]{2,1,0:T(8,128)(2,1)S(1)}, f32[128]{0:T(128)S(1)}) custom-call(s32[3,768]{1,0:T(4,128)} %miller_hbm.1, f32[3]{0:T(128)} %kpoint_hbm.1, bf16[2,128,768]{2,1,0:T(8,128)(2,1)} %waves_ref.1, s32[16]{0:T(128)} %species_hbm.1, s32[16]{0:T(128)} %counts_hbm.1, s32[3,16]{1,0:T(4,128)} %positions_hbm.1, f32[4,8,16]{2,1,0:T(8,128)} %radial_hbm.1, ...), custom_call_target="tpu_custom_call" | custom-call | tf_op jit(solution)/shard_map/pallas_call | solution.py:325
  14.2 0.7 %copy.12 = bf16[2,128,768]{2,1,0:T(8,128)(2,1)} copy(bf16[2,128,768]{2,1,0:T(8,128)(2,1)S(1)} %get-tuple-element.2) | data formatting | bytes 786432
  14.9 0.5 %copy.13 = f32[128]{0:T(128)} copy(f32[128]{0:T(128)S(1)} %get-tuple-element.3) | data formatting | bytes 1024

commit v3 on v2

--- a/solution.py
+++ b/solution.py
@@ -11,7 +11,8 @@
 
 PROJ = 8
 MGRID = 64
-ATOM_BLOCK = 16
+SPLIT = 2
+ATOM_BLOCK = 8
 
 
 def turn_polynomials(degree=8):
@@ -40,12 +41,16 @@
 
 
 def peers_of(me, n, body):
+    def one(peer):
+        @pl.when(peer != me)
+        def _():
+            body(peer)
+
     if n <= 32:
-        order = sorted(range(1, n), key=lambda k: -min(k, n - k))
-        for k in order:
-            body(lax.rem(me + k, n))
+        for peer in sorted(range(n), key=lambda p: (p // 2 % 2, p)):
+            one(peer)
     else:
-        lax.fori_loop(1, n, lambda k, c: (body(lax.rem(me + k, n)), c)[1], 0)
+        repeat(n, one)
 
 
 def repeat(count, body):
@@ -105,6 +110,8 @@
     rank = (me - base) // stride
     is_owner = (me >= base) & (rank < q) & (lax.rem(me - base + n * stride, stride) == 0)
     mine_rank = jnp.clip(rank, 0, q - 1)
+    halves_n = recv.shape[0]
+    share = own // halves_n
     bands = waves_ref.shape[1]
     planes = waves_ref.shape[2]
     species_n, _, terms = radial_hbm.shape
@@ -182,8 +189,6 @@
                 at = pl.multiple_of(at, 2 * PROJ)
             bbuf[pl.ds(at, 2 * PROJ), :] = both.astype(bbuf.dtype)
 
-    loop(atoms // ATOM_BLOCK, build)
-    wave_copy.wait()
     height = ATOM_BLOCK * 2 * PROJ
 
     def intersect(block):
@@ -203,84 +208,112 @@
         part[pl.ds(block * ATOM_BLOCK, ATOM_BLOCK)] = over
         send[pl.ds(block * ATOM_BLOCK, ATOM_BLOCK)] = over.astype(send.dtype)
 
-    loop(atoms // ATOM_BLOCK, intersect)
-    pl.semaphore_wait(barrier, n - 1)
 
     def many_of(ref, count, sem):
         view = ref.at[pl.ds(0, count)]
         return pltpu.make_async_copy(view, view, sem)
 
-    def scatter(o):
+    def scatter(h, o):
         peer = base + o * stride
 
         @pl.when(peer != me)
         def _():
             pltpu.make_async_remote_copy(
-                src_ref=send.at[pl.ds(o * own, own)],
-                dst_ref=recv.at[me],
+                src_ref=send.at[pl.ds(h * (atoms // halves_n) + o * share, share)],
+                dst_ref=recv.at[h, me],
                 send_sem=send_sems.at[0],
-                recv_sem=recv_sems.at[0],
+                recv_sem=recv_sems.at[h],
                 device_id={"ga": peer},
                 device_id_type=pl.DeviceIdType.MESH,
             ).start()
 
-    repeat(q, scatter)
+    blocks = atoms // ATOM_BLOCK
+    if blocks == halves_n:
+        for h in range(halves_n):
+            build(h)
+            if h == 0:
+                wave_copy.wait()
+            intersect(h)
+            if h == 0:
+                pl.semaphore_wait(barrier, n - 1)
+            repeat(q, functools.partial(scatter, h))
+    else:
+        loop(blocks, build)
+        wave_copy.wait()
+        loop(blocks, intersect)
+        pl.semaphore_wait(barrier, n - 1)
+        for h in range(halves_n):
+            repeat(q, functools.partial(scatter, h))
 
     @pl.when(is_owner)
     def _():
-        recv[me] = jnp.zeros((own, 2 * PROJ, bands), recv.dtype)
         columns = []
-        for k in range(own):
-            mine = lax.broadcasted_iota(jnp.int32, (PROJ, atoms), 1) == mine_rank * own + k
-            columns.append(
-                [
-                    jnp.broadcast_to(
-                        jnp.sum(jnp.where(mine, coupling_ref[j], 0.0), axis=1, keepdims=True),
-                        (PROJ, bands),
-                    )
-                    for j in range(PROJ)
-                ]
-            )
-        many_of(recv, n - 1, recv_sems.at[0]).wait()
-        energy = jnp.zeros((1, bands), f32)
-        for k in range(own):
-            over = part[mine_rank * own + k]
-            for p in range(n):
-                over = over + recv[p, k].astype(f32)
-            weighted = []
-            for half in range(2):
-                piece = over[half * PROJ : (half + 1) * PROJ]
-                total = columns[k][0] * piece[0:1]
-                for j in range(1, PROJ):
-                    total = total + columns[k][j] * piece[j : j + 1]
-                energy = energy + jnp.sum(total * piece, axis=0, keepdims=True)
-                weighted.append(total)
-            wbuf[mine_rank, k] = jnp.concatenate(weighted, axis=0).astype(wbuf.dtype)
-        ebuf[mine_rank] = energy
-
-        def spread(buffer, index):
+        for h in range(halves_n):
+            recv[h, me] = jnp.zeros((share, 2 * PROJ, bands), recv.dtype)
+        for h in range(halves_n):
+            for k in range(share):
+                atom = h * (atoms // halves_n) + mine_rank * share + k
+                mine = lax.broadcasted_iota(jnp.int32, (PROJ, atoms), 1) == atom
+                columns.append(
+                    [
+                        jnp.broadcast_to(
+                            jnp.sum(jnp.where(mine, coupling_ref[j], 0.0), axis=1, keepdims=True),
+                            (PROJ, bands),
+                        )
+                        for j in range(PROJ)
+                    ]
+                )
+
+        def spread(source, target, send_sem, recv_sem):
             def copy(peer):
                 pltpu.make_async_remote_copy(
-                    src_ref=buffer.at[mine_rank],
-                    dst_ref=buffer.at[mine_rank],
-                    send_sem=send_sems.at[index],
-                    recv_sem=recv_sems.at[index],
+                    src_ref=source,
+                    dst_ref=target,
+                    send_sem=send_sem,
+                    recv_sem=recv_sem,
                     device_id={"ga": peer},
                     device_id_type=pl.DeviceIdType.MESH,
                 ).start()
 
             return copy
 
-        peers_of(me, n, spread(wbuf, 1))
-        peers_of(me, n, spread(ebuf, 2))
+        energy = jnp.zeros((1, bands), f32)
+        for h in range(halves_n):
+            many_of(recv.at[h], n - 1, recv_sems.at[h]).wait()
+            for k in range(share):
+                over = part[h * (atoms // halves_n) + mine_rank * share + k]
+                for p in range(n):
+                    over = over + recv[h, p, k].astype(f32)
+                weighted = []
+                for half in range(2):
+                    piece = over[half * PROJ : (half + 1) * PROJ]
+                    total = columns[h * share + k][0] * piece[0:1]
+                    for j in range(1, PROJ):
+                        total = total + columns[h * share + k][j] * piece[j : j + 1]
+                    energy = energy + jnp.sum(total * piece, axis=0, keepdims=True)
+                    weighted.append(total)
+                wbuf[h, mine_rank, k] = jnp.concatenate(weighted, axis=0).astype(wbuf.dtype)
+            mine_w = wbuf.at[h, mine_rank]
+            peers_of(
+                me, n, spread(mine_w, mine_w, send_sems.at[1 + h], recv_sems.at[halves_n + h])
+            )
+        ebuf[mine_rank] = energy
+        mine_e = ebuf.at[mine_rank]
+        peers_of(
+            me,
+            n,
+            spread(mine_e, mine_e, send_sems.at[1 + halves_n], recv_sems.at[2 * halves_n]),
+        )
         many_of(send, (q - 1) * own, send_sems.at[0]).wait()
         if q > 1:
-            many_of(wbuf, q - 1, recv_sems.at[1]).wait()
+            for h in range(halves_n):
+                many_of(wbuf.at[h], q - 1, recv_sems.at[halves_n + h]).wait()
 
     @pl.when(jnp.logical_not(is_owner))
     def _():
         many_of(send, q * own, send_sems.at[0]).wait()
-        many_of(wbuf, q, recv_sems.at[1]).wait()
+        for h in range(halves_n):
+            many_of(wbuf.at[h], q, recv_sems.at[halves_n + h]).wait()
 
     weights = wbuf[...].reshape(atoms, 2 * PROJ, bands).astype(f32)
     upper, lower = weights[:, :PROJ], weights[:, PROJ:]
@@ -297,18 +330,19 @@
     @pl.when(is_owner)
     def _():
         if q > 1:
-            many_of(ebuf, q - 1, recv_sems.at[2]).wait()
+            many_of(ebuf, q - 1, recv_sems.at[2 * halves_n]).wait()
 
     @pl.when(jnp.logical_not(is_owner))
     def _():
-        many_of(ebuf, q, recv_sems.at[2]).wait()
+        many_of(ebuf, q, recv_sems.at[2 * halves_n]).wait()
 
     energy_ref[...] = jnp.sum(ebuf[...], axis=(0, 1)) / (atoms * PROJ)
 
     @pl.when(is_owner)
     def _():
-        for index, buffer in ((1, recv), (2, tally)):
-            many_of(buffer, n - 1, send_sems.at[index]).wait()
+        for h in range(halves_n):
+            many_of(recv.at[h], n - 1, send_sems.at[1 + h]).wait()
+        many_of(tally, n - 1, send_sems.at[1 + halves_n]).wait()
 
 
 def on_device(miller_index, kpoint, waves, species, counts, positions, radial_coef, coupling):
@@ -318,6 +352,7 @@
     scaling = 1.0 / math.sqrt(planes * n)
     q = owners_of(n, atoms)[0]
     own = atoms // q
+    halves_n = SPLIT if own % SPLIT == 0 else 1
     vmem = pl.BlockSpec(memory_space=pltpu.VMEM)
     smem = pl.BlockSpec(memory_space=pltpu.SMEM)
     anywhere = pl.BlockSpec(memory_space=pl.ANY)
@@ -337,13 +372,13 @@
             pltpu.VMEM((radial_coef.shape[0], PROJ, planes), f32),
             pltpu.VMEM((atoms, 2 * PROJ, bands), f32),
             pltpu.VMEM((atoms, 2 * PROJ, bands), bf16),
-            pltpu.VMEM((n, own, 2 * PROJ, bands), bf16),
-            pltpu.VMEM((q, own, 2 * PROJ, bands), bf16),
+            pltpu.VMEM((halves_n, n, own // halves_n, 2 * PROJ, bands), bf16),
+            pltpu.VMEM((halves_n, q, own // halves_n, 2 * PROJ, bands), bf16),
             pltpu.VMEM((q, 1, bands), f32),
             pltpu.VMEM((n, 1, bands), f32),
             pltpu.SemaphoreType.DMA,
-            pltpu.SemaphoreType.DMA((3,)),
-            pltpu.SemaphoreType.DMA((3,)),
+            pltpu.SemaphoreType.DMA((2 + halves_n,)),
+            pltpu.SemaphoreType.DMA((1 + 2 * halves_n,)),
             pltpu.VMEM(miller_index.shape, jnp.int32),
             pltpu.SMEM(kpoint.shape, f32),
             pltpu.SMEM(species.shape, jnp.int32),

time: 15.6 us -> 15.3 us (0.981)
  Pallas kernels: 13.5 us -> 13.2 us
    pallas_call x1, Pallas kernels: 13.5 us -> 13.2 us  [on_device(): pl.pallas_call(functools.partial(kernel, n, scaling), out_shape=(pltpu.VM...]
where the time goes in v3:
time: 15.3 us; the launch traced here: 15.1 us
  Pallas kernels  13.2 us (86%)
  local copies, waits for them, and re-layouts  1.26 us (8%)
  between operations  0.64 us (4%)
    pallas_call x1, Pallas kernels, on_device(): pl.pallas_call(functools.partial(kernel, n, scaling), out_shape=(pltpu.VM...  13.2 us
    unnamed x2, local copies, waits for them, and re-layouts  1.26 us

profile of v3, /device:TPU:0, one launch (start us, length us, event | category | flops | bytes accessed | tf_op | source)
XLA Modules:
  0.0 15.1 jit_solution(7939941881430835922)
XLA Ops:
  0.6 13.2 %shard_map.95 = (bf16[2,128,768]{2,1,0:T(8,128)(2,1)S(1)}, f32[128]{0:T(128)S(1)}) custom-call(s32[3,768]{1,0:T(4,128)} %miller_hbm.1, f32[3]{0:T(128)} %kpoint_hbm.1, bf16[2,128,768]{2,1,0:T(8,128)(2,1)} %waves_ref.1, s32[16]{0:T(128)} %species_hbm.1, s32[16]{0:T(128)} %counts_hbm.1, s32[3,16]{1,0:T(4,128)} %positions_hbm.1, f32[4,8,16]{2,1,0:T(8,128)} %radial_hbm.1, ...), custom_call_target="tpu_custom_call" | custom-call | tf_op jit(solution)/shard_map/pallas_call | solution.py:360
  13.8 0.7 %copy.12 = bf16[2,128,768]{2,1,0:T(8,128)(2,1)} copy(bf16[2,128,768]{2,1,0:T(8,128)(2,1)S(1)} %get-tuple-element.2) | data formatting | bytes 786432
  14.6 0.5 %copy.13 = f32[128]{0:T(128)} copy(f32[128]{0:T(128)S(1)} %get-tuple-element.3) | data formatting | bytes 1024
